TPU v7x, 512 devices: a whole 4x8x8 slice. The times are simulated.
512 devices in a mesh: grp: 16 (over y, core), mem: 32 (over x, z).
Axes of the slice: x: 4, y: 8, z: 8, core: 2. Of those that a mesh axis runs over, the one named last changes fastest.
Arguments:
- v_stack: bfloat16 [524288, 512], P(('grp', 'mem')), may hold values from -0.1875 to 0.1875
- u_stack: bfloat16 [524288, 512], P(('grp', 'mem')), may hold values from -0.25 to 0.25
- warm_start: bfloat16 [524288, 256], P(('grp', 'mem')), may hold values from -3 to 3
- observed: bfloat16 [524288, 256], P(('grp', 'mem')), may hold values from -12 to 12, as said below
- owners: int32 [512, 4], replicated, may hold values from 0 to 511, as said below
- tile_ranks: int32 [512, 4], P(('grp', 'mem')), may hold values from 8 to 128
Outputs:
- model: float32 [524288, 256], P(('grp', 'mem'))
- residual: bfloat16 [524288, 256], P(('grp', 'mem'))
Inputs may be any that keep to these rules, and one draw needn't show every extreme that they name: Writing d = g * 32 + m, owners[d, t] = ((g + a_t) mod 16) * 32 + (m + b_t) mod 32, where the offsets a_t differ over t, the offsets b_t differ over t, some slot has a_t = 15, some slot has a_t = 8, some slot has b_t = 31 and some slot has b_t = 16. `observed`: entries of one row block share a scale.
All inputs are finite; a program needn't handle non-finite values.
Results may differ from a plain program's by a relative error of at most 0.006.
Values may be sent and summed in bfloat16 or wider, within the bound.
No kernel may reach another device: no remote copies, remote signals or barrier semaphores. Data moves between devices by JAX's collectives and lax.ppermute only.
A program may use at most 64 MiB of HBM per device.

v0:
```python
import functools

import jax
import jax.numpy as jnp
from jax import lax
from jax.experimental import pallas as pl
from jax.experimental.pallas import tpu as pltpu
from jax.sharding import Mesh
from jax.sharding import PartitionSpec as P

ITERS = 2
ALL = ("y", "c", "x", "z")
GRP = ("y", "c")
MEM = ("x", "z")
LANES = 128
PAIR = 2
F32 = jnp.float32
BF16 = jnp.bfloat16


def call(kernel, out_shape, in_spaces, scratch=(), flops=0, vmem_mib=12):
    spaces = {"v": pltpu.VMEM, "s": pltpu.SMEM}
    return pl.pallas_call(
        kernel,
        out_shape=out_shape,
        in_specs=[pl.BlockSpec(memory_space=spaces[s]) for s in in_spaces],
        out_specs=jax.tree.map(lambda _: pl.BlockSpec(memory_space=pltpu.VMEM), out_shape),
        scratch_shapes=list(scratch),
        compiler_params=pltpu.CompilerParams(vmem_limit_bytes=vmem_mib * 2**20),
        cost_estimate=pl.CostEstimate(flops=flops, bytes_accessed=2**20, transcendentals=0),
    )


def panel_of(ref, slot, cap, kind, column):
    pairs = cap // PAIR
    slots = ref.shape[0] // (2 * pairs)
    first = ((column % 2) * slots + slot) * pairs
    return ref[first : first + pairs, kind + column // 2].reshape(cap, LANES)


def rows_of(ref, slot, cap, kind, columns):
    return jnp.concatenate([panel_of(ref, slot, cap, kind, c) for c in range(columns)], axis=1)


def put_pieces(out_ref, first, rows):
    half = out_ref.shape[0] // 2
    pairs = rows.shape[0] // PAIR
    for h in range(2):
        piece = rows[:, h * LANES : (h + 1) * LANES].reshape(pairs, PAIR, LANES)
        out_ref[h * half + first : h * half + first + pairs] = piece


def move(outer, inner, leads, shifts, src_ref, put, double_ref):
    def widen(o, carry):
        rows = src_ref[pl.ds(o * inner, inner)]
        double_ref[pl.ds(2 * o * inner, inner)] = rows
        double_ref[pl.ds((2 * o + 1) * inner, inner)] = rows
        return carry

    lax.fori_loop(0, outer, widen, 0)

    def rows(o, carry):
        for k, (lead, shift) in enumerate(zip(leads, shifts)):
            start = 2 * o * inner + ((inner - shift) & (inner - 1))
            put(k, ((o + lead) & (outer - 1)) * inner, double_ref[pl.ds(start, inner)])
        return carry

    lax.fori_loop(0, outer, rows, 0)


def deliver_kernel(outer, inner, owner_ref, here_ref, src_ref, out_ref, double_ref):
    owner = owner_ref[here_ref[0]]

    def put(k, first, rows):
        out_ref[pl.ds(first, inner)] = rows

    move(
        outer, inner, [lax.div(owner, inner)], [lax.rem(owner, inner)], src_ref, put, double_ref
    )


def exchange_kernel(outer, inner, slots, owner_ref, here_ref, src_ref, out_ref, double_ref):
    slot = here_ref[0]
    group = lax.div(owner_ref[slot], inner)
    member = lax.rem(owner_ref[slot], inner)
    leads = [outer - group]
    shifts = [inner - member]
    for k in range(1, slots):
        other = owner_ref[lax.rem(slot + k, slots)]
        leads.append(lax.div(other, inner) - group + outer)
        shifts.append((lax.rem(other, inner) - member + inner) & (inner - 1))

    def put(k, first, rows):
        out_ref[pl.ds(first, inner), k] = rows

    move(outer, inner, leads, shifts, src_ref, put, double_ref)


def keep_live(rows, limit):
    row = lax.broadcasted_iota(jnp.int32, rows.shape, 0)
    return jnp.where(row < limit, rows, jnp.zeros_like(rows))


def spread_kernel(got_ref, out_ref):
    sums = jnp.sum(got_ref[...], axis=0, keepdims=True)
    out_ref[...] = jnp.broadcast_to(sums, out_ref.shape)


def huber_scale(sums_ref, entries):
    spread = jnp.sum(sums_ref[:, 0, :], axis=0, keepdims=True)
    return 1.345 * spread[:, 0:1] / entries + 1e-06


def first_kernel(
    cap, pieces_ref, u_ref, observed_ref, residual_ref, sums_ref, gram_ref, arrived_ref
):
    for t in range(u_ref.shape[1] // cap):
        arrived_ref[t * cap : (t + 1) * cap] = rows_of(pieces_ref, t, cap, 0, 2)
        gram_ref[t * cap : (t + 1) * cap] = rows_of(pieces_ref, t, cap, 1, gram_ref.shape[1] // LANES)
    total = jnp.zeros((1, 1), F32)
    step = 256
    for i in range(0, u_ref.shape[0], step):
        rows = jnp.dot(u_ref[i : i + step], arrived_ref[...], preferred_element_type=F32)
        rows = rows - observed_ref[i : i + step].astype(F32)
        residual_ref[i : i + step] = rows
        total = total + jnp.sum(jnp.abs(rows), keepdims=True)
    sums_ref[...] = jnp.broadcast_to(total[None], sums_ref.shape)


def weigh_kernel(entries, sums_ref, residual_ref, ut_ref, pieces_ref, own_ref, weighted_ref):
    scale = huber_scale(sums_ref, entries)
    residual = residual_ref[...]
    weighted_ref[...] = (scale / jnp.maximum(jnp.abs(residual), scale) * residual).astype(BF16)
    step = 256
    for i in range(0, ut_ref.shape[0], step):
        rows = jnp.dot(ut_ref[i : i + step], weighted_ref[...], preferred_element_type=F32)
        rows = rows.astype(BF16)
        own_ref[i : i + step] = rows
        put_pieces(pieces_ref, i // PAIR, rows)


def iterate_kernel(
    cap,
    entries,
    ranks_ref,
    spread_ref,
    pieces_ref,
    own_ref,
    gram_ref,
    v_ref,
    u_ref,
    residual_ref,
    gradient_ref,
    image_ref,
    sums_ref,
    back_ref,
    around_ref,
    panels_ref,
):
    slots = v_ref.shape[1] // cap
    step = 256
    for t in range(slots):
        back_ref[t * cap : (t + 1) * cap] = keep_live(rows_of(pieces_ref, t, cap, 0, 2), ranks_ref[t])
    grad = jnp.zeros((1, 1), F32)
    for i in range(0, v_ref.shape[0], step):
        rows = jnp.dot(v_ref[i : i + step], back_ref[...], preferred_element_type=F32)
        gradient_ref[i : i + step] = rows
        grad = grad + jnp.sum(rows * rows, keepdims=True)
    for mine in range(slots):
        for t in range(slots):
            kind = (mine - t) % slots
            if kind == 0:
                around_ref[t * cap : (t + 1) * cap] = own_ref[t * cap : (t + 1) * cap]
            else:
                around_ref[t * cap : (t + 1) * cap] = rows_of(pieces_ref, t, cap, kind, 2)
        panels_ref[mine * cap : (mine + 1) * cap] = jnp.dot(
            gram_ref[mine * cap : (mine + 1) * cap], around_ref[...], preferred_element_type=F32
        ).astype(BF16)
    scale = huber_scale(spread_ref, entries)
    curve = jnp.zeros((1, 1), F32)
    for i in range(0, u_ref.shape[0], step):
        rows = jnp.dot(u_ref[i : i + step], panels_ref[...], preferred_element_type=F32)
        image_ref[i : i + step] = rows
        weights = scale / jnp.maximum(jnp.abs(residual_ref[i : i + step]), scale)
        curve = curve + jnp.sum(weights * rows * rows, keepdims=True)
    sums_ref[:, 0:1, :] = jnp.broadcast_to(grad[None], (sums_ref.shape[0], 1, LANES))
    sums_ref[:, 1:2, :] = jnp.broadcast_to(curve[None], (sums_ref.shape[0], 1, LANES))


def step_of(sums_ref):
    grad = jnp.sum(sums_ref[:, 0, :], axis=0, keepdims=True)[:, 0:1]
    curve = jnp.sum(sums_ref[:, 1, :], axis=0, keepdims=True)[:, 0:1]
    return grad / (curve + 1e-06)


def update_kernel(sums_ref, residual_ref, image_ref, out_ref, step_ref, spread_ref):
    step = step_of(sums_ref)
    residual = residual_ref[...] - step * image_ref[...]
    out_ref[...] = residual
    step_ref[...] = jnp.broadcast_to(step, step_ref.shape)
    total = jnp.sum(jnp.abs(residual), keepdims=True)
    spread_ref[...] = jnp.broadcast_to(total[None], spread_ref.shape)


def last_kernel(sums_ref, residual_ref, image_ref, start_ref, gradient_ref, *rest):
    earlier, (out_ref, residual_out_ref) = rest[:-2], rest[-2:]
    step = step_of(sums_ref)
    model = start_ref[...].astype(F32)
    for k in range(0, len(earlier), 2):
        model = model - earlier[k][0:1, 0:1] * earlier[k + 1][...]
    out_ref[...] = model - step * gradient_ref[...]
    residual_out_ref[...] = (residual_ref[...] - step * image_ref[...]).astype(BF16)


def on_device(v_stack, u_stack, warm_start, observed, owners, tile_ranks):
    groups = lax.axis_size(GRP)
    members = lax.axis_size(MEM)
    devices = groups * members
    slots = owners.shape[1]
    block, width = v_stack.shape
    cap = width // slots
    rhs = warm_start.shape[1]
    entries = float(block * rhs * groups * members)
    ranks = tile_ranks[0]
    struct = jax.ShapeDtypeStruct
    field = struct((block, rhs), F32)
    rounded = struct((block, rhs), BF16)
    panels_shape = struct((width, rhs), BF16)
    piece = (PAIR, LANES)
    flops = 2 * block * width * rhs

    half = devices // 2
    slot = lax.axis_index(ALL) % half // (half // slots)
    here = slot[None]
    owner = owners[0]

    def scatter(x, axes):
        return lax.all_to_all(x, axes, split_axis=0, concat_axis=0, tiled=True)

    def route(kernel, pieces, out):
        got = scatter(pieces, ALL)
        moved = call(
            functools.partial(kernel, groups, members),
            struct((devices,) + out, BF16),
            "ssv",
            [pltpu.VMEM((2 * devices,) + pieces.shape[1:], BF16)],
            flops=10**8,
        )(owner, here, got)
        return scatter(moved, ALL)

    def total(partial):
        got = scatter(partial, GRP)
        kinds = partial.shape[1]
        spread = call(spread_kernel, struct((members, kinds, LANES), F32), "v")(got)
        return scatter(spread, MEM)

    live = (
        lax.broadcasted_iota(jnp.int32, (slots, cap), 1) < ranks[:, None]
    ).reshape(width)
    ut = u_stack.T
    products = lax.dot_general(
        v_stack,
        jnp.concatenate([warm_start, v_stack], axis=1),
        (((0,), (0,)), ((), ())),
        preferred_element_type=F32,
    )
    columns = jnp.concatenate([jnp.ones((rhs,), jnp.bool_), live])
    products = jnp.where(live[:, None] & columns[None, :], products, 0.0).astype(BF16)
    kinds = (rhs + width) // (2 * LANES)
    pieces = (
        products.reshape(width // PAIR, PAIR, kinds, 2, LANES)
        .transpose(3, 0, 2, 1, 4)
        .reshape((devices, kinds) + piece)
    )
    one = struct((groups, 1, LANES), F32)
    two = struct((groups, 2, LANES), F32)
    residual, partial, gram = call(
        functools.partial(first_kernel, cap),
        (field, one, struct((width, width), BF16)),
        "vvv",
        [pltpu.VMEM((width, rhs), BF16)],
        flops=flops,
    )(route(deliver_kernel, pieces, (kinds,) + piece), u_stack, observed)
    exchange = lambda outer, inner, *refs: exchange_kernel(outer, inner, slots, *refs)
    earlier = []
    for index in range(ITERS):
        spread = total(partial)
        pieces, own = call(
            functools.partial(weigh_kernel, entries),
            (struct((devices,) + piece, BF16), panels_shape),
            "vvv",
            [pltpu.VMEM((block, rhs), BF16)],
            flops=flops,
        )(spread, residual, ut)
        gradient, image, partial = call(
            functools.partial(iterate_kernel, cap, entries),
            (field, field, two),
            "svvvvvvv",
            [pltpu.VMEM((width, rhs), BF16)] * 3,
            flops=3 * flops,
        )(
            ranks,
            spread,
            route(exchange, pieces, (slots,) + piece),
            own,
            gram,
            v_stack,
            u_stack,
            residual,
        )
        sums = total(partial)
        if index < ITERS - 1:
            residual, step, partial = call(
                update_kernel, (field, struct((8, LANES), F32), one), "vvv"
            )(sums, residual, image)
            earlier += [step, gradient]
        else:
            model, residual = call(last_kernel, (field, rounded), "v" * (5 + len(earlier)))(
                sums, residual, image, warm_start, gradient, *earlier
            )
    return model, residual


def solution(mesh):
    finer = Mesh(mesh.devices.reshape(8, 2, 4, 8), ALL)
    rows = P(ALL, None)
    return jax.shard_map(
        on_device,
        mesh=finer,
        in_specs=(rows, rows, rows, rows, P(), rows),
        out_specs=(rows, rows),
        check_vma=False,
    )
```

profile of v0, /device:TPU:1, one launch (start us, length us, event | category | flops | bytes accessed | tf_op | source)
XLA Modules:
  0.0 343.4 jit_solution(16345367017501560734)
XLA Ops:
  1.4 2.7 fusion.4
  4.5 1.5 copy.11
  6.0 22.1 %all-to-all-start = ((bf16[512,3,2,128]{3,2,1,0:T(2,128)(2,1)}), bf16[512,3,2,128]{3,2,1,0:T(2,128)(2,1)S(1)}, u32[]{:S(2)}, u32[]{:S(2)}) async-start(bf16[512,3,2,128]{3,2,1,0:T(2,128)(2,1)} %bitcast.5), calls=%async_computation | async-start | bytes 1572864 | tf_op jit(solution)/shard_map/all_to_all | solution.py:238
  29.0 26.2 %all-to-all-done.src_ref = bf16[512,3,2,128]{3,2,1,0:T(2,128)(2,1)S(1)} async-done(((bf16[512,3,2,128]{3,2,1,0:T(2,128)(2,1)}), bf16[512,3,2,128]{3,2,1,0:T(2,128)(2,1)S(1)}, u32[]{:S(2)}, u32[]{:S(2)}) %all-to-all-start) | async-done | bytes 786464 | tf_op jit(solution)/shard_map/all_to_all | solution.py:238
  55.2 1.5 shard_map.77
  56.8 37.5 %all_to_all.70.pieces_ref = bf16[512,3,2,128]{3,2,1,0:T(2,128)(2,1)S(1)} all-to-all(bf16[512,3,2,128]{3,2,1,0:T(2,128)(2,1)S(1)} %shard_map.77), channel_id=1, replica_groups=mesh['y'=8,'c'=2,'x'=4,'z'=8] {'y','c','x','z'}, dimensions={0} | all-to-all | bytes 1572864 | tf_op jit(solution)/shard_map/all_to_all | solution.py:238
  95.9 11.1 %all_to_all.71.got_ref = f32[16,1,128]{2,1,0:T(1,128)S(1)} all-to-all(f32[16,1,128]{2,1,0:T(1,128)S(1)} %get-tuple-element.18), channel_id=1, replica_groups=mesh['y'=8,'c'=2,'x'=4,'z'=8] {'y','c'}, dimensions={0} | all-to-all | bytes 16384 | tf_op jit(solution)/shard_map/all_to_all | solution.py:238
  107.6 4.4 %all-to-all-start.3 = ((f32[32,1,128]{2,1,0:T(1,128)}), f32[32,1,128]{2,1,0:T(1,128)S(1)}, u32[]{:S(2)}, u32[]{:S(2)}) async-start(f32[32,1,128]{2,1,0:T(1,128)} %shard_map.79), calls=%async_computation.3 | async-start | bytes 32768 | tf_op jit(solution)/shard_map/all_to_all | solution.py:238
  112.5 8.0 %all-to-all-done.3.sums_ref.spread_ref = f32[32,1,128]{2,1,0:T(1,128)S(1)} async-done(((f32[32,1,128]{2,1,0:T(1,128)}), f32[32,1,128]{2,1,0:T(1,128)S(1)}, u32[]{:S(2)}, u32[]{:S(2)}) %all-to-all-start.3) | async-done | bytes 16416 | tf_op jit(solution)/shard_map/all_to_all | solution.py:238
  121.3 27.8 %all_to_all.72.refs_2_ = bf16[512,2,128]{2,1,0:T(2,128)(2,1)S(1)} all-to-all(bf16[512,2,128]{2,1,0:T(2,128)(2,1)S(1)} %get-tuple-element.20), channel_id=1, replica_groups=mesh['y'=8,'c'=2,'x'=4,'z'=8] {'y','c','x','z'}, dimensions={0} | all-to-all | bytes 524288 | tf_op jit(solution)/shard_map/all_to_all | solution.py:238
  149.0 1.8 shard_map.81
  150.8 42.8 %all_to_all.73.pieces_ref = bf16[512,4,2,128]{3,2,1,0:T(2,128)(2,1)S(1)} all-to-all(bf16[512,4,2,128]{3,2,1,0:T(2,128)(2,1)S(1)} %shard_map.81), channel_id=1, replica_groups=mesh['y'=8,'c'=2,'x'=4,'z'=8] {'y','c','x','z'}, dimensions={0} | all-to-all | bytes 2097152 | tf_op jit(solution)/shard_map/all_to_all | solution.py:238
  193.6 1.9 shard_map.82
  195.6 11.0 %all_to_all.74.got_ref = f32[16,2,128]{2,1,0:T(2,128)S(1)} all-to-all(f32[16,2,128]{2,1,0:T(2,128)S(1)} %get-tuple-element.23), channel_id=1, replica_groups=mesh['y'=8,'c'=2,'x'=4,'z'=8] {'y','c'}, dimensions={0} | all-to-all | bytes 32768 | tf_op jit(solution)/shard_map/all_to_all | solution.py:238
  206.6 12.9 %all_to_all.75.sums_ref = f32[32,2,128]{2,1,0:T(2,128)S(1)} all-to-all(f32[32,2,128]{2,1,0:T(2,128)S(1)} %shard_map.83), channel_id=1, replica_groups=mesh['y'=8,'c'=2,'x'=4,'z'=8] {'x','z'}, dimensions={0} | all-to-all | bytes 65536 | tf_op jit(solution)/shard_map/all_to_all | solution.py:238
  220.2 11.3 %all_to_all.76.got_ref = f32[16,1,128]{2,1,0:T(1,128)S(1)} all-to-all(f32[16,1,128]{2,1,0:T(1,128)S(1)} %get-tuple-element.25), channel_id=1, replica_groups=mesh['y'=8,'c'=2,'x'=4,'z'=8] {'y','c'}, dimensions={0} | all-to-all | bytes 16384 | tf_op jit(solution)/shard_map/all_to_all | solution.py:238
  231.5 11.6 %all_to_all.77.sums_ref.spread_ref = f32[32,1,128]{2,1,0:T(1,128)S(1)} all-to-all(f32[32,1,128]{2,1,0:T(1,128)S(1)} %shard_map.85), channel_id=1, replica_groups=mesh['y'=8,'c'=2,'x'=4,'z'=8] {'x','z'}, dimensions={0} | all-to-all | bytes 32768 | tf_op jit(solution)/shard_map/all_to_all | solution.py:238
  243.8 27.3 %all_to_all.78.refs_2_ = bf16[512,2,128]{2,1,0:T(2,128)(2,1)S(1)} all-to-all(bf16[512,2,128]{2,1,0:T(2,128)(2,1)S(1)} %get-tuple-element.27), channel_id=1, replica_groups=mesh['y'=8,'c'=2,'x'=4,'z'=8] {'y','c','x','z'}, dimensions={0} | all-to-all | bytes 524288 | tf_op jit(solution)/shard_map/all_to_all | solution.py:238
  271.1 1.8 shard_map.87
  272.9 42.9 %all_to_all.79.pieces_ref = bf16[512,4,2,128]{3,2,1,0:T(2,128)(2,1)S(1)} all-to-all(bf16[512,4,2,128]{3,2,1,0:T(2,128)(2,1)S(1)} %shard_map.87), channel_id=1, replica_groups=mesh['y'=8,'c'=2,'x'=4,'z'=8] {'y','c','x','z'}, dimensions={0} | all-to-all | bytes 2097152 | tf_op jit(solution)/shard_map/all_to_all | solution.py:238
  315.8 2.1 shard_map.88
  317.9 11.0 %all_to_all.80.got_ref = f32[16,2,128]{2,1,0:T(2,128)S(1)} all-to-all(f32[16,2,128]{2,1,0:T(2,128)S(1)} %get-tuple-element.29), channel_id=1, replica_groups=mesh['y'=8,'c'=2,'x'=4,'z'=8] {'y','c'}, dimensions={0} | all-to-all | bytes 32768 | tf_op jit(solution)/shard_map/all_to_all | solution.py:238
  328.9 12.9 %all_to_all.81.sums_ref = f32[32,2,128]{2,1,0:T(2,128)S(1)} all-to-all(f32[32,2,128]{2,1,0:T(2,128)S(1)} %shard_map.89), channel_id=1, replica_groups=mesh['y'=8,'c'=2,'x'=4,'z'=8] {'x','z'}, dimensions={0} | all-to-all | bytes 65536 | tf_op jit(solution)/shard_map/all_to_all | solution.py:238
  341.8 1.6 shard_map.90
  (28 shorter events, 6.9 us)
Async XLA Ops:
  6.0 49.2 %all-to-all-start = ((bf16[512,3,2,128]{3,2,1,0:T(2,128)(2,1)}), bf16[512,3,2,128]{3,2,1,0:T(2,128)(2,1)S(1)}, u32[]{:S(2)}, u32[]{:S(2)}) async-start(bf16[512,3,2,128]{3,2,1,0:T(2,128)(2,1)} %bitcast.5), calls=%async_computation | async-start | bytes 1572864 | tf_op jit(solution)/shard_map/all_to_all | solution.py:238
  56.7 37.5 %copy-start = (bf16[1024,512]{1,0:T(8,128)(2,1)S(1)}, bf16[1024,512]{1,0:T(8,128)(2,1)}, u32[]{:S(2)}) copy-start(bf16[1024,512]{1,0:T(8,128)(2,1)} %u_ref.5) | copy-start | bytes 3145732
  56.8 37.5 %copy-start.4 = (bf16[1024,256]{1,0:T(8,128)(2,1)S(1)}, bf16[1024,256]{1,0:T(8,128)(2,1)}, u32[]{:S(2)}) copy-start(bf16[1024,256]{1,0:T(8,128)(2,1)} %observed_ref.1) | copy-start | bytes 1572868
  95.1 0.8 copy-start.2
  107.6 13.0 %all-to-all-start.3 = ((f32[32,1,128]{2,1,0:T(1,128)}), f32[32,1,128]{2,1,0:T(1,128)S(1)}, u32[]{:S(2)}, u32[]{:S(2)}) async-start(f32[32,1,128]{2,1,0:T(1,128)} %shard_map.79), calls=%async_computation.3 | async-start | bytes 32768 | tf_op jit(solution)/shard_map/all_to_all | solution.py:238
  150.8 42.8 %copy-start.1 = (bf16[1024,512]{1,0:T(8,128)(2,1)S(1)}, bf16[1024,512]{1,0:T(8,128)(2,1)}, u32[]{:S(2)}) copy-start(bf16[1024,512]{1,0:T(8,128)(2,1)} %v_ref.3) | copy-start | bytes 3145732
  150.8 42.8 %copy-start.3 = (bf16[512,512]{1,0:T(8,128)(2,1)S(1)}, bf16[512,512]{1,0:T(8,128)(2,1)}, u32[]{:S(2)}) copy-start(bf16[512,512]{1,0:T(8,128)(2,1)} %copy-done.2) | copy-start | bytes 1572868
  150.8 42.8 %copy-start.6 = (s32[1,4]{1,0:T(1,128)S(1)}, s32[1,4]{1,0:T(1,128)}, u32[]{:S(2)}) copy-start(s32[1,4]{1,0:T(1,128)} %param.11) | copy-start | bytes 52
  315.8 26.0 %copy-start.5 = (bf16[1024,256]{1,0:T(8,128)(2,1)S(1)}, bf16[1024,256]{1,0:T(8,128)(2,1)}, u32[]{:S(2)}) copy-start(bf16[1024,256]{1,0:T(8,128)(2,1)} %start_ref.1) | copy-start | bytes 1572868
where the time goes:
time: 344 us; the launch traced here: 343 us
  blocking collectives  260 us (76%)
  waiting for transfers between devices  34.2 us (10%)
  starting transfers between devices  26.5 us (8%)
  Pallas kernels  14.2 us (4%)
  local copies, waits for them, and re-layouts  4.1 us (1%)
    all_to_all x12, blocking collectives, scatter(): return lax.all_to_all(x, axes, split_axis=0, concat_axis=0, tiled=True)  260 us
    all_to_all x2, waiting for transfers between devices, scatter(): return lax.all_to_all(x, axes, split_axis=0, concat_axis=0, tiled=True)  34.2 us
    all_to_all x2, starting transfers between devices, scatter(): return lax.all_to_all(x, axes, split_axis=0, concat_axis=0, tiled=True)  26.5 us
  transfers between devices with their start and end apart: 2, of which 2 were waited for; matrix products, arithmetic and copies ran while one was open for 0% of the time, Pallas kernels for 0%

commit v1 on v0

--- a/solution.py
+++ b/solution.py
@@ -111,9 +111,33 @@
     return 1.345 * spread[:, 0:1] / entries + 1e-06
 
 
+def start_kernel(cap, ranks_ref, v_ref, warm_ref, pieces_ref):
+    slots = v_ref.shape[1] // cap
+    kinds = pieces_ref.shape[1]
+    half = pieces_ref.shape[0] // 2
+    pairs = cap // PAIR
+    for t in range(slots):
+        vt = v_ref[:, t * cap : (t + 1) * cap].T
+        for kind in range(kinds):
+            if kind == 0:
+                right = warm_ref[...]
+            else:
+                right = v_ref[:, (kind - 1) * 2 * LANES : kind * 2 * LANES]
+            rows = keep_live(jnp.dot(vt, right, preferred_element_type=F32), ranks_ref[t])
+            for h in range(2):
+                part = rows[:, h * LANES : (h + 1) * LANES]
+                if kind > 0:
+                    column = ((kind - 1) * 2 + h) * LANES
+                    lane = lax.broadcasted_iota(jnp.int32, part.shape, 1) + column % cap
+                    part = jnp.where(lane < ranks_ref[column // cap], part, jnp.zeros_like(part))
+                first = h * half + t * pairs
+                pieces_ref[first : first + pairs, kind] = part.astype(BF16).reshape(pairs, PAIR, LANES)
+
+
 def first_kernel(
-    cap, pieces_ref, u_ref, observed_ref, residual_ref, sums_ref, gram_ref, arrived_ref
+    cap, pieces_ref, u_ref, observed_ref, residual_ref, sums_ref, gram_ref, ut_ref, arrived_ref
 ):
+    ut_ref[...] = u_ref[...].T
     for t in range(u_ref.shape[1] // cap):
         arrived_ref[t * cap : (t + 1) * cap] = rows_of(pieces_ref, t, cap, 0, 2)
         gram_ref[t * cap : (t + 1) * cap] = rows_of(pieces_ref, t, cap, 1, gram_ref.shape[1] // LANES)
@@ -183,14 +207,13 @@
         image_ref[i : i + step] = rows
         weights = scale / jnp.maximum(jnp.abs(residual_ref[i : i + step]), scale)
         curve = curve + jnp.sum(weights * rows * rows, keepdims=True)
-    sums_ref[:, 0:1, :] = jnp.broadcast_to(grad[None], (sums_ref.shape[0], 1, LANES))
-    sums_ref[:, 1:2, :] = jnp.broadcast_to(curve[None], (sums_ref.shape[0], 1, LANES))
+    lane = lax.broadcasted_iota(jnp.int32, sums_ref.shape, 2)
+    sums_ref[...] = jnp.where(lane < LANES // 2, grad[None], curve[None])
 
 
 def step_of(sums_ref):
-    grad = jnp.sum(sums_ref[:, 0, :], axis=0, keepdims=True)[:, 0:1]
-    curve = jnp.sum(sums_ref[:, 1, :], axis=0, keepdims=True)[:, 0:1]
-    return grad / (curve + 1e-06)
+    sums = jnp.sum(sums_ref[:, 0, :], axis=0, keepdims=True)
+    return sums[:, 0:1] / (sums[:, LANES // 2 : LANES // 2 + 1] + 1e-06)
 
 
 def update_kernel(sums_ref, residual_ref, image_ref, out_ref, step_ref, spread_ref):
@@ -250,33 +273,20 @@
 
     def total(partial):
         got = scatter(partial, GRP)
-        kinds = partial.shape[1]
-        spread = call(spread_kernel, struct((members, kinds, LANES), F32), "v")(got)
+        spread = call(spread_kernel, struct((members, 1, LANES), F32), "v")(got)
         return scatter(spread, MEM)
 
-    live = (
-        lax.broadcasted_iota(jnp.int32, (slots, cap), 1) < ranks[:, None]
-    ).reshape(width)
-    ut = u_stack.T
-    products = lax.dot_general(
-        v_stack,
-        jnp.concatenate([warm_start, v_stack], axis=1),
-        (((0,), (0,)), ((), ())),
-        preferred_element_type=F32,
-    )
-    columns = jnp.concatenate([jnp.ones((rhs,), jnp.bool_), live])
-    products = jnp.where(live[:, None] & columns[None, :], products, 0.0).astype(BF16)
     kinds = (rhs + width) // (2 * LANES)
-    pieces = (
-        products.reshape(width // PAIR, PAIR, kinds, 2, LANES)
-        .transpose(3, 0, 2, 1, 4)
-        .reshape((devices, kinds) + piece)
-    )
+    pieces = call(
+        functools.partial(start_kernel, cap),
+        struct((devices, kinds) + piece, BF16),
+        "svv",
+        flops=3 * flops,
+    )(ranks, v_stack, warm_start)
     one = struct((groups, 1, LANES), F32)
-    two = struct((groups, 2, LANES), F32)
-    residual, partial, gram = call(
+    residual, partial, gram, ut = call(
         functools.partial(first_kernel, cap),
-        (field, one, struct((width, width), BF16)),
+        (field, one, struct((width, width), BF16), struct((width, block), BF16)),
         "vvv",
         [pltpu.VMEM((width, rhs), BF16)],
         flops=flops,
@@ -294,7 +304,7 @@
         )(spread, residual, ut)
         gradient, image, partial = call(
             functools.partial(iterate_kernel, cap, entries),
-            (field, field, two),
+            (field, field, one),
             "svvvvvvv",
             [pltpu.VMEM((width, rhs), BF16)] * 3,
             flops=3 * flops,

time: 344 us -> 342 us (level)
  blocking collectives: 260 us -> 272 us
  waiting for transfers between devices: 34.2 us -> 26.2 us
  starting transfers between devices: 26.5 us -> 22.2 us
    all_to_all x12 -> x13, blocking collectives: 260 us -> 272 us  [scatter(): return lax.all_to_all(x, axes, split_axis=0, concat_axis=0, tiled=True)]
    all_to_all x2 -> x1, waiting for transfers between devices: 34.2 us -> 26.2 us  [scatter(): return lax.all_to_all(x, axes, split_axis=0, concat_axis=0, tiled=True)]
    all_to_all x2 -> x1, starting transfers between devices: 26.5 us -> 22.2 us  [scatter(): return lax.all_to_all(x, axes, split_axis=0, concat_axis=0, tiled=True)]
  transfers between devices with their start and end apart: 2 -> 1, of which waited for: 2 -> 1; matrix products, arithmetic and copies ran while one was open for 0% -> 0% of each run, Pallas kernels for 0% -> 0%
where the time goes in v1:
time: 342 us; the launch traced here: 341 us
  blocking collectives  272 us (80%)
  waiting for transfers between devices  26.2 us (8%)
  starting transfers between devices  22.2 us (6%)
  Pallas kernels  16.4 us (5%)
  local copies, waits for them, and re-layouts  3.73 us (1%)
    all_to_all x13, blocking collectives, scatter(): return lax.all_to_all(x, axes, split_axis=0, concat_axis=0, tiled=True)  272 us
    all_to_all x1, waiting for transfers between devices, scatter(): return lax.all_to_all(x, axes, split_axis=0, concat_axis=0, tiled=True)  26.2 us
    all_to_all x1, starting transfers between devices, scatter(): return lax.all_to_all(x, axes, split_axis=0, concat_axis=0, tiled=True)  22.2 us
  transfers between devices with their start and end apart: 1, of which 1 were waited for; matrix products, arithmetic and copies ran while one was open for 0% of the time, Pallas kernels for 0%

profile of v1, /device:TPU:1, one launch (start us, length us, event | category | flops | bytes accessed | tf_op | source)
XLA Modules:
  0.0 341.4 jit_solution(8891775565805050101)
XLA Ops:
  1.3 1.2 copy-done.1
  2.5 1.0 copy-done.4
  3.6 2.7 shard_map.77
  6.3 22.2 %all-to-all-start = ((bf16[512,3,2,128]{3,2,1,0:T(2,128)(2,1)}), bf16[512,3,2,128]{3,2,1,0:T(2,128)(2,1)S(1)}, u32[]{:S(2)}, u32[]{:S(2)}) async-start(bf16[512,3,2,128]{3,2,1,0:T(2,128)(2,1)} %shard_map.77), calls=%async_computation | async-start | bytes 1572864 | tf_op jit(solution)/shard_map/all_to_all | solution.py:261
  29.3 26.2 %all-to-all-done.src_ref = bf16[512,3,2,128]{3,2,1,0:T(2,128)(2,1)S(1)} async-done(((bf16[512,3,2,128]{3,2,1,0:T(2,128)(2,1)}), bf16[512,3,2,128]{3,2,1,0:T(2,128)(2,1)S(1)}, u32[]{:S(2)}, u32[]{:S(2)}) %all-to-all-start) | async-done | bytes 786464 | tf_op jit(solution)/shard_map/all_to_all | solution.py:261
  55.4 1.5 shard_map.78
  57.0 37.5 %all_to_all.70.pieces_ref = bf16[512,3,2,128]{3,2,1,0:T(2,128)(2,1)S(1)} all-to-all(bf16[512,3,2,128]{3,2,1,0:T(2,128)(2,1)S(1)} %shard_map.78), channel_id=1, replica_groups=mesh['y'=8,'c'=2,'x'=4,'z'=8] {'y','c','x','z'}, dimensions={0} | all-to-all | bytes 1572864 | tf_op jit(solution)/shard_map/all_to_all | solution.py:261
  95.4 11.1 %all_to_all.71.got_ref = f32[16,1,128]{2,1,0:T(1,128)S(1)} all-to-all(f32[16,1,128]{2,1,0:T(1,128)S(1)} %get-tuple-element.19), channel_id=1, replica_groups=mesh['y'=8,'c'=2,'x'=4,'z'=8] {'y','c'}, dimensions={0} | all-to-all | bytes 16384 | tf_op jit(solution)/shard_map/all_to_all | solution.py:261
  106.5 12.8 %all_to_all.72.sums_ref.spread_ref = f32[32,1,128]{2,1,0:T(1,128)S(1)} all-to-all(f32[32,1,128]{2,1,0:T(1,128)S(1)} %shard_map.80), channel_id=1, replica_groups=mesh['y'=8,'c'=2,'x'=4,'z'=8] {'x','z'}, dimensions={0} | all-to-all | bytes 32768 | tf_op jit(solution)/shard_map/all_to_all | solution.py:261
  120.1 27.6 %all_to_all.73.refs_2_ = bf16[512,2,128]{2,1,0:T(2,128)(2,1)S(1)} all-to-all(bf16[512,2,128]{2,1,0:T(2,128)(2,1)S(1)} %get-tuple-element.22), channel_id=1, replica_groups=mesh['y'=8,'c'=2,'x'=4,'z'=8] {'y','c','x','z'}, dimensions={0} | all-to-all | bytes 524288 | tf_op jit(solution)/shard_map/all_to_all | solution.py:261
  147.6 1.8 shard_map.82
  149.4 43.0 %all_to_all.74.pieces_ref = bf16[512,4,2,128]{3,2,1,0:T(2,128)(2,1)S(1)} all-to-all(bf16[512,4,2,128]{3,2,1,0:T(2,128)(2,1)S(1)} %shard_map.82), channel_id=1, replica_groups=mesh['y'=8,'c'=2,'x'=4,'z'=8] {'y','c','x','z'}, dimensions={0} | all-to-all | bytes 2097152 | tf_op jit(solution)/shard_map/all_to_all | solution.py:261
  192.4 2.0 shard_map.83
  194.4 10.7 %all_to_all.75.got_ref = f32[16,1,128]{2,1,0:T(1,128)S(1)} all-to-all(f32[16,1,128]{2,1,0:T(1,128)S(1)} %get-tuple-element.25), channel_id=1, replica_groups=mesh['y'=8,'c'=2,'x'=4,'z'=8] {'y','c'}, dimensions={0} | all-to-all | bytes 16384 | tf_op jit(solution)/shard_map/all_to_all | solution.py:261
  205.2 12.8 %all_to_all.76.sums_ref = f32[32,1,128]{2,1,0:T(1,128)S(1)} all-to-all(f32[32,1,128]{2,1,0:T(1,128)S(1)} %shard_map.84), channel_id=1, replica_groups=mesh['y'=8,'c'=2,'x'=4,'z'=8] {'x','z'}, dimensions={0} | all-to-all | bytes 32768 | tf_op jit(solution)/shard_map/all_to_all | solution.py:261
  218.6 11.6 %all_to_all.77.got_ref = f32[16,1,128]{2,1,0:T(1,128)S(1)} all-to-all(f32[16,1,128]{2,1,0:T(1,128)S(1)} %get-tuple-element.27), channel_id=1, replica_groups=mesh['y'=8,'c'=2,'x'=4,'z'=8] {'y','c'}, dimensions={0} | all-to-all | bytes 16384 | tf_op jit(solution)/shard_map/all_to_all | solution.py:261
  230.2 11.6 %all_to_all.78.sums_ref.spread_ref = f32[32,1,128]{2,1,0:T(1,128)S(1)} all-to-all(f32[32,1,128]{2,1,0:T(1,128)S(1)} %shard_map.86), channel_id=1, replica_groups=mesh['y'=8,'c'=2,'x'=4,'z'=8] {'x','z'}, dimensions={0} | all-to-all | bytes 32768 | tf_op jit(solution)/shard_map/all_to_all | solution.py:261
  242.5 27.3 %all_to_all.79.refs_2_ = bf16[512,2,128]{2,1,0:T(2,128)(2,1)S(1)} all-to-all(bf16[512,2,128]{2,1,0:T(2,128)(2,1)S(1)} %get-tuple-element.29), channel_id=1, replica_groups=mesh['y'=8,'c'=2,'x'=4,'z'=8] {'y','c','x','z'}, dimensions={0} | all-to-all | bytes 524288 | tf_op jit(solution)/shard_map/all_to_all | solution.py:261
  269.8 1.8 shard_map.88
  271.6 42.7 %all_to_all.80.pieces_ref = bf16[512,4,2,128]{3,2,1,0:T(2,128)(2,1)S(1)} all-to-all(bf16[512,4,2,128]{3,2,1,0:T(2,128)(2,1)S(1)} %shard_map.88), channel_id=1, replica_groups=mesh['y'=8,'c'=2,'x'=4,'z'=8] {'y','c','x','z'}, dimensions={0} | all-to-all | bytes 2097152 | tf_op jit(solution)/shard_map/all_to_all | solution.py:261
  314.3 2.0 shard_map.89
  316.3 10.7 %all_to_all.81.got_ref = f32[16,1,128]{2,1,0:T(1,128)S(1)} all-to-all(f32[16,1,128]{2,1,0:T(1,128)S(1)} %get-tuple-element.31), channel_id=1, replica_groups=mesh['y'=8,'c'=2,'x'=4,'z'=8] {'y','c'}, dimensions={0} | all-to-all | bytes 16384 | tf_op jit(solution)/shard_map/all_to_all | solution.py:261
  327.0 12.8 %all_to_all.82.sums_ref = f32[32,1,128]{2,1,0:T(1,128)S(1)} all-to-all(f32[32,1,128]{2,1,0:T(1,128)S(1)} %shard_map.90), channel_id=1, replica_groups=mesh['y'=8,'c'=2,'x'=4,'z'=8] {'x','z'}, dimensions={0} | all-to-all | bytes 32768 | tf_op jit(solution)/shard_map/all_to_all | solution.py:261
  339.8 1.6 shard_map.91
  (21 shorter events, 4.5 us)
Async XLA Ops:
  0.6 0.7 copy-start.6
  1.3 1.2 copy-start.1
  2.5 1.0 copy-start.4
  6.3 49.2 %all-to-all-start = ((bf16[512,3,2,128]{3,2,1,0:T(2,128)(2,1)}), bf16[512,3,2,128]{3,2,1,0:T(2,128)(2,1)S(1)}, u32[]{:S(2)}, u32[]{:S(2)}) async-start(bf16[512,3,2,128]{3,2,1,0:T(2,128)(2,1)} %shard_map.77), calls=%async_computation | async-start | bytes 1572864 | tf_op jit(solution)/shard_map/all_to_all | solution.py:261
  57.0 37.5 %copy-start = (bf16[1024,512]{1,0:T(8,128)(2,1)S(1)}, bf16[1024,512]{1,0:T(8,128)(2,1)}, u32[]{:S(2)}) copy-start(bf16[1024,512]{1,0:T(8,128)(2,1)} %u_ref.5) | copy-start | bytes 3145732
  57.0 37.5 %copy-start.3 = (bf16[1024,256]{1,0:T(8,128)(2,1)S(1)}, bf16[1024,256]{1,0:T(8,128)(2,1)}, u32[]{:S(2)}) copy-start(bf16[1024,256]{1,0:T(8,128)(2,1)} %observed_ref.1) | copy-start | bytes 1572868
  149.4 43.0 %copy-start.2 = (bf16[1024,512]{1,0:T(8,128)(2,1)S(1)}, bf16[1024,512]{1,0:T(8,128)(2,1)}, u32[]{:S(2)}) copy-start(bf16[1024,512]{1,0:T(8,128)(2,1)} %v_ref.5) | copy-start | bytes 3145732
  314.3 25.5 %copy-start.5 = (bf16[1024,256]{1,0:T(8,128)(2,1)S(1)}, bf16[1024,256]{1,0:T(8,128)(2,1)}, u32[]{:S(2)}) copy-start(bf16[1024,256]{1,0:T(8,128)(2,1)} %start_ref.1) | copy-start | bytes 1572868

commit v2 on v1

--- a/solution.py
+++ b/solution.py
@@ -19,14 +19,14 @@
 
 
 def call(kernel, out_shape, in_spaces, scratch=(), flops=0, vmem_mib=12):
-    spaces = {"v": pltpu.VMEM, "s": pltpu.SMEM}
+    spaces = {"v": pltpu.VMEM, "s": pltpu.SMEM, "h": pltpu.HBM}
     return pl.pallas_call(
         kernel,
         out_shape=out_shape,
         in_specs=[pl.BlockSpec(memory_space=spaces[s]) for s in in_spaces],
         out_specs=jax.tree.map(lambda _: pl.BlockSpec(memory_space=pltpu.VMEM), out_shape),
         scratch_shapes=list(scratch),
-        compiler_params=pltpu.CompilerParams(vmem_limit_bytes=vmem_mib * 2**20),
+        compiler_params=pltpu.CompilerParams(vmem_limit_bytes=int(vmem_mib * 2**20)),
         cost_estimate=pl.CostEstimate(flops=flops, bytes_accessed=2**20, transcendentals=0),
     )
 
@@ -111,27 +111,36 @@
     return 1.345 * spread[:, 0:1] / entries + 1e-06
 
 
-def start_kernel(cap, ranks_ref, v_ref, warm_ref, pieces_ref):
+def start_kernel(
+    cap, ranks_ref, v_hbm_ref, warm_hbm_ref, pieces_ref, v_ref, warm_ref, vt_ref, sems
+):
+    load_v = pltpu.make_async_copy(v_hbm_ref, v_ref, sems.at[0])
+    load_warm = pltpu.make_async_copy(warm_hbm_ref, warm_ref, sems.at[1])
+    load_v.start()
+    load_warm.start()
+    load_v.wait()
+    vt_ref[...] = v_ref[...].T
     slots = v_ref.shape[1] // cap
-    kinds = pieces_ref.shape[1]
     half = pieces_ref.shape[0] // 2
     pairs = cap // PAIR
-    for t in range(slots):
-        vt = v_ref[:, t * cap : (t + 1) * cap].T
-        for kind in range(kinds):
-            if kind == 0:
-                right = warm_ref[...]
-            else:
-                right = v_ref[:, (kind - 1) * 2 * LANES : kind * 2 * LANES]
-            rows = keep_live(jnp.dot(vt, right, preferred_element_type=F32), ranks_ref[t])
+
+    def put(kind, right):
+        rows = jnp.dot(vt_ref[...], right, preferred_element_type=F32)
+        for t in range(slots):
             for h in range(2):
-                part = rows[:, h * LANES : (h + 1) * LANES]
+                part = rows[t * cap : (t + 1) * cap, h * LANES : (h + 1) * LANES]
+                part = keep_live(part, ranks_ref[t])
                 if kind > 0:
                     column = ((kind - 1) * 2 + h) * LANES
                     lane = lax.broadcasted_iota(jnp.int32, part.shape, 1) + column % cap
                     part = jnp.where(lane < ranks_ref[column // cap], part, jnp.zeros_like(part))
                 first = h * half + t * pairs
                 pieces_ref[first : first + pairs, kind] = part.astype(BF16).reshape(pairs, PAIR, LANES)
+
+    for kind in range(1, pieces_ref.shape[1]):
+        put(kind, v_ref[:, (kind - 1) * 2 * LANES : kind * 2 * LANES])
+    load_warm.wait()
+    put(0, warm_ref[...])
 
 
 def first_kernel(
@@ -280,8 +289,15 @@
     pieces = call(
         functools.partial(start_kernel, cap),
         struct((devices, kinds) + piece, BF16),
-        "svv",
+        "shh",
+        [
+            pltpu.VMEM((block, width), BF16),
+            pltpu.VMEM((block, rhs), BF16),
+            pltpu.VMEM((width, block), BF16),
+            pltpu.SemaphoreType.DMA((2,)),
+        ],
         flops=3 * flops,
+        vmem_mib=60.5,
     )(ranks, v_stack, warm_start)
     one = struct((groups, 1, LANES), F32)
     residual, partial, gram, ut = call(

time: 342 us -> 342 us (level)
  no operation moved by 1% of the time
where the time goes in v2:
time: 342 us; the launch traced here: 341 us
  blocking collectives  272 us (80%)
  waiting for transfers between devices  26.2 us (8%)
  starting transfers between devices  22.2 us (6%)
  Pallas kernels  18.2 us (5%)
    all_to_all x13, blocking collectives, scatter(): return lax.all_to_all(x, axes, split_axis=0, concat_axis=0, tiled=True)  272 us
    all_to_all x1, waiting for transfers between devices, scatter(): return lax.all_to_all(x, axes, split_axis=0, concat_axis=0, tiled=True)  26.2 us
    all_to_all x1, starting transfers between devices, scatter(): return lax.all_to_all(x, axes, split_axis=0, concat_axis=0, tiled=True)  22.2 us
  transfers between devices with their start and end apart: 1, of which 1 were waited for; matrix products, arithmetic and copies ran while one was open for 0% of the time, Pallas kernels for 0%

profile of v2, /device:TPU:1, one launch (start us, length us, event | category | flops | bytes accessed | tf_op | source)
XLA Modules:
  0.0 341.0 jit_solution(11720000553662148623)
XLA Ops:
  0.6 4.6 %shard_map.77 = bf16[512,3,2,128]{3,2,1,0:T(2,128)(2,1)} custom-call(s32[4]{0:T(128)} %bitcast.2, bf16[1024,512]{1,0:T(8,128)(2,1)} %v_ref.3, bf16[1024,256]{1,0:T(8,128)(2,1)} %start_ref.1), custom_call_target="tpu_custom_call" | custom-call | flops 805306368 | bytes 1048576 | tf_op jit(solution)/shard_map/pallas_call | solution.py:289
  5.3 22.2 %all-to-all-start = ((bf16[512,3,2,128]{3,2,1,0:T(2,128)(2,1)}), bf16[512,3,2,128]{3,2,1,0:T(2,128)(2,1)S(1)}, u32[]{:S(2)}, u32[]{:S(2)}) async-start(bf16[512,3,2,128]{3,2,1,0:T(2,128)(2,1)} %shard_map.77), calls=%async_computation | async-start | bytes 1572864 | tf_op jit(solution)/shard_map/all_to_all | solution.py:270
  27.5 0.8 slice_reduce_fusion.owner_ref.refs_0_
  28.3 26.2 %all-to-all-done.src_ref = bf16[512,3,2,128]{3,2,1,0:T(2,128)(2,1)S(1)} async-done(((bf16[512,3,2,128]{3,2,1,0:T(2,128)(2,1)}), bf16[512,3,2,128]{3,2,1,0:T(2,128)(2,1)S(1)}, u32[]{:S(2)}, u32[]{:S(2)}) %all-to-all-start) | async-done | bytes 786464 | tf_op jit(solution)/shard_map/all_to_all | solution.py:270
  54.4 1.5 shard_map.78
  56.0 37.5 %all_to_all.70.pieces_ref = bf16[512,3,2,128]{3,2,1,0:T(2,128)(2,1)S(1)} all-to-all(bf16[512,3,2,128]{3,2,1,0:T(2,128)(2,1)S(1)} %shard_map.78), channel_id=1, replica_groups=mesh['y'=8,'c'=2,'x'=4,'z'=8] {'y','c','x','z'}, dimensions={0} | all-to-all | bytes 1572864 | tf_op jit(solution)/shard_map/all_to_all | solution.py:270
  93.5 0.9 shard_map.79
  94.3 11.1 %all_to_all.71.got_ref = f32[16,1,128]{2,1,0:T(1,128)S(1)} all-to-all(f32[16,1,128]{2,1,0:T(1,128)S(1)} %get-tuple-element.19), channel_id=1, replica_groups=mesh['y'=8,'c'=2,'x'=4,'z'=8] {'y','c'}, dimensions={0} | all-to-all | bytes 16384 | tf_op jit(solution)/shard_map/all_to_all | solution.py:270
  105.5 12.9 %all_to_all.72.sums_ref.spread_ref = f32[32,1,128]{2,1,0:T(1,128)S(1)} all-to-all(f32[32,1,128]{2,1,0:T(1,128)S(1)} %shard_map.80), channel_id=1, replica_groups=mesh['y'=8,'c'=2,'x'=4,'z'=8] {'x','z'}, dimensions={0} | all-to-all | bytes 32768 | tf_op jit(solution)/shard_map/all_to_all | solution.py:270
  119.0 27.6 %all_to_all.73.refs_2_ = bf16[512,2,128]{2,1,0:T(2,128)(2,1)S(1)} all-to-all(bf16[512,2,128]{2,1,0:T(2,128)(2,1)S(1)} %get-tuple-element.22), channel_id=1, replica_groups=mesh['y'=8,'c'=2,'x'=4,'z'=8] {'y','c','x','z'}, dimensions={0} | all-to-all | bytes 524288 | tf_op jit(solution)/shard_map/all_to_all | solution.py:270
  146.6 1.8 shard_map.82
  148.4 43.0 %all_to_all.74.pieces_ref = bf16[512,4,2,128]{3,2,1,0:T(2,128)(2,1)S(1)} all-to-all(bf16[512,4,2,128]{3,2,1,0:T(2,128)(2,1)S(1)} %shard_map.82), channel_id=1, replica_groups=mesh['y'=8,'c'=2,'x'=4,'z'=8] {'y','c','x','z'}, dimensions={0} | all-to-all | bytes 2097152 | tf_op jit(solution)/shard_map/all_to_all | solution.py:270
  192.0 2.0 shard_map.83
  194.0 10.7 %all_to_all.75.got_ref = f32[16,1,128]{2,1,0:T(1,128)S(1)} all-to-all(f32[16,1,128]{2,1,0:T(1,128)S(1)} %get-tuple-element.25), channel_id=1, replica_groups=mesh['y'=8,'c'=2,'x'=4,'z'=8] {'y','c'}, dimensions={0} | all-to-all | bytes 16384 | tf_op jit(solution)/shard_map/all_to_all | solution.py:270
  204.7 12.8 %all_to_all.76.sums_ref = f32[32,1,128]{2,1,0:T(1,128)S(1)} all-to-all(f32[32,1,128]{2,1,0:T(1,128)S(1)} %shard_map.84), channel_id=1, replica_groups=mesh['y'=8,'c'=2,'x'=4,'z'=8] {'x','z'}, dimensions={0} | all-to-all | bytes 32768 | tf_op jit(solution)/shard_map/all_to_all | solution.py:270
  218.2 11.6 %all_to_all.77.got_ref = f32[16,1,128]{2,1,0:T(1,128)S(1)} all-to-all(f32[16,1,128]{2,1,0:T(1,128)S(1)} %get-tuple-element.27), channel_id=1, replica_groups=mesh['y'=8,'c'=2,'x'=4,'z'=8] {'y','c'}, dimensions={0} | all-to-all | bytes 16384 | tf_op jit(solution)/shard_map/all_to_all | solution.py:270
  229.8 11.6 %all_to_all.78.sums_ref.spread_ref = f32[32,1,128]{2,1,0:T(1,128)S(1)} all-to-all(f32[32,1,128]{2,1,0:T(1,128)S(1)} %shard_map.86), channel_id=1, replica_groups=mesh['y'=8,'c'=2,'x'=4,'z'=8] {'x','z'}, dimensions={0} | all-to-all | bytes 32768 | tf_op jit(solution)/shard_map/all_to_all | solution.py:270
  242.2 27.3 %all_to_all.79.refs_2_ = bf16[512,2,128]{2,1,0:T(2,128)(2,1)S(1)} all-to-all(bf16[512,2,128]{2,1,0:T(2,128)(2,1)S(1)} %get-tuple-element.29), channel_id=1, replica_groups=mesh['y'=8,'c'=2,'x'=4,'z'=8] {'y','c','x','z'}, dimensions={0} | all-to-all | bytes 524288 | tf_op jit(solution)/shard_map/all_to_all | solution.py:270
  269.5 1.8 shard_map.88
  271.2 42.7 %all_to_all.80.pieces_ref = bf16[512,4,2,128]{3,2,1,0:T(2,128)(2,1)S(1)} all-to-all(bf16[512,4,2,128]{3,2,1,0:T(2,128)(2,1)S(1)} %shard_map.88), channel_id=1, replica_groups=mesh['y'=8,'c'=2,'x'=4,'z'=8] {'y','c','x','z'}, dimensions={0} | all-to-all | bytes 2097152 | tf_op jit(solution)/shard_map/all_to_all | solution.py:270
  313.9 1.9 shard_map.89
  315.8 10.7 %all_to_all.81.got_ref = f32[16,1,128]{2,1,0:T(1,128)S(1)} all-to-all(f32[16,1,128]{2,1,0:T(1,128)S(1)} %get-tuple-element.31), channel_id=1, replica_groups=mesh['y'=8,'c'=2,'x'=4,'z'=8] {'y','c'}, dimensions={0} | all-to-all | bytes 16384 | tf_op jit(solution)/shard_map/all_to_all | solution.py:270
  326.6 12.8 %all_to_all.82.sums_ref = f32[32,1,128]{2,1,0:T(1,128)S(1)} all-to-all(f32[32,1,128]{2,1,0:T(1,128)S(1)} %shard_map.90), channel_id=1, replica_groups=mesh['y'=8,'c'=2,'x'=4,'z'=8] {'x','z'}, dimensions={0} | all-to-all | bytes 32768 | tf_op jit(solution)/shard_map/all_to_all | solution.py:270
  339.4 1.6 shard_map.91
  (17 shorter events, 2.8 us)
Async XLA Ops:
  5.3 49.2 %all-to-all-start = ((bf16[512,3,2,128]{3,2,1,0:T(2,128)(2,1)}), bf16[512,3,2,128]{3,2,1,0:T(2,128)(2,1)S(1)}, u32[]{:S(2)}, u32[]{:S(2)}) async-start(bf16[512,3,2,128]{3,2,1,0:T(2,128)(2,1)} %shard_map.77), calls=%async_computation | async-start | bytes 1572864 | tf_op jit(solution)/shard_map/all_to_all | solution.py:270
  56.0 37.5 %copy-start = (bf16[1024,512]{1,0:T(8,128)(2,1)S(1)}, bf16[1024,512]{1,0:T(8,128)(2,1)}, u32[]{:S(2)}) copy-start(bf16[1024,512]{1,0:T(8,128)(2,1)} %u_ref.5) | copy-start | bytes 3145732
  56.0 37.5 %copy-start.2 = (bf16[1024,256]{1,0:T(8,128)(2,1)S(1)}, bf16[1024,256]{1,0:T(8,128)(2,1)}, u32[]{:S(2)}) copy-start(bf16[1024,256]{1,0:T(8,128)(2,1)} %observed_ref.1) | copy-start | bytes 1572868
  148.4 43.0 %copy-start.1 = (bf16[1024,512]{1,0:T(8,128)(2,1)S(1)}, bf16[1024,512]{1,0:T(8,128)(2,1)}, u32[]{:S(2)}) copy-start(bf16[1024,512]{1,0:T(8,128)(2,1)} %v_ref.3) | copy-start | bytes 3145732
  191.4 0.7 copy-start.4
  313.9 25.5 %copy-start.3 = (bf16[1024,256]{1,0:T(8,128)(2,1)S(1)}, bf16[1024,256]{1,0:T(8,128)(2,1)}, u32[]{:S(2)}) copy-start(bf16[1024,256]{1,0:T(8,128)(2,1)} %start_ref.1) | copy-start | bytes 1572868

commit v3 on v2

--- a/solution.py
+++ b/solution.py
@@ -50,50 +50,53 @@
         out_ref[h * half + first : h * half + first + pairs] = piece
 
 
-def move(outer, inner, leads, shifts, src_ref, put, double_ref):
-    def widen(o, carry):
-        rows = src_ref[pl.ds(o * inner, inner)]
-        double_ref[pl.ds(2 * o * inner, inner)] = rows
-        double_ref[pl.ds((2 * o + 1) * inner, inner)] = rows
+def widen(outer, inner, src_ref, double_ref):
+    def rows(o, carry):
+        block = src_ref[pl.ds(o * inner, inner)]
+        double_ref[pl.ds(2 * o * inner, inner)] = block
+        double_ref[pl.ds((2 * o + 1) * inner, inner)] = block
         return carry
 
-    lax.fori_loop(0, outer, widen, 0)
-
-    def rows(o, carry):
-        for k, (lead, shift) in enumerate(zip(leads, shifts)):
-            start = 2 * o * inner + ((inner - shift) & (inner - 1))
-            put(k, ((o + lead) & (outer - 1)) * inner, double_ref[pl.ds(start, inner)])
-        return carry
-
     lax.fori_loop(0, outer, rows, 0)
+
+
+def arriving(outer, inner, o, lead, shift, double_ref):
+    source = (o + outer - lead) & (outer - 1)
+    return double_ref[pl.ds(2 * source * inner + ((inner - shift) & (inner - 1)), inner)]
 
 
 def deliver_kernel(outer, inner, owner_ref, here_ref, src_ref, out_ref, double_ref):
     owner = owner_ref[here_ref[0]]
-
-    def put(k, first, rows):
-        out_ref[pl.ds(first, inner)] = rows
-
-    move(
-        outer, inner, [lax.div(owner, inner)], [lax.rem(owner, inner)], src_ref, put, double_ref
-    )
+    lead, shift = lax.div(owner, inner), lax.rem(owner, inner)
+    widen(outer, inner, src_ref, double_ref)
+
+    def rows(o, carry):
+        out_ref[pl.ds(o * inner, inner)] = arriving(outer, inner, o, lead, shift, double_ref)
+        return carry
+
+    lax.fori_loop(0, outer, rows, 0)
 
 
 def exchange_kernel(outer, inner, slots, owner_ref, here_ref, src_ref, out_ref, double_ref):
     slot = here_ref[0]
     group = lax.div(owner_ref[slot], inner)
     member = lax.rem(owner_ref[slot], inner)
-    leads = [outer - group]
-    shifts = [inner - member]
+    leads = [(outer - group) & (outer - 1)]
+    shifts = [(inner - member) & (inner - 1)]
     for k in range(1, slots):
         other = owner_ref[lax.rem(slot + k, slots)]
-        leads.append(lax.div(other, inner) - group + outer)
+        leads.append((lax.div(other, inner) - group + outer) & (outer - 1))
         shifts.append((lax.rem(other, inner) - member + inner) & (inner - 1))
-
-    def put(k, first, rows):
-        out_ref[pl.ds(first, inner), k] = rows
-
-    move(outer, inner, leads, shifts, src_ref, put, double_ref)
+    widen(outer, inner, src_ref, double_ref)
+
+    def rows(o, carry):
+        pieces = [
+            arriving(outer, inner, o, lead, shift, double_ref) for lead, shift in zip(leads, shifts)
+        ]
+        out_ref[pl.ds(o * inner, inner)] = jnp.concatenate(pieces, axis=1)
+        return carry
+
+    lax.fori_loop(0, outer, rows, 0)
 
 
 def keep_live(rows, limit):
@@ -327,7 +330,7 @@
         )(
             ranks,
             spread,
-            route(exchange, pieces, (slots,) + piece),
+            route(exchange, pieces, (slots * PAIR, LANES)).reshape((devices, slots) + piece),
             own,
             gram,
             v_stack,

time: 342 us -> 342 us (level)
  no operation moved by 1% of the time
where the time goes in v3:
time: 342 us; the launch traced here: 341 us
  blocking collectives  272 us (80%)
  waiting for transfers between devices  26.2 us (8%)
  starting transfers between devices  22.2 us (6%)
  Pallas kernels  18.2 us (5%)
    all_to_all x13, blocking collectives, scatter(): return lax.all_to_all(x, axes, split_axis=0, concat_axis=0, tiled=True)  272 us
    all_to_all x1, waiting for transfers between devices, scatter(): return lax.all_to_all(x, axes, split_axis=0, concat_axis=0, tiled=True)  26.2 us
    all_to_all x1, starting transfers between devices, scatter(): return lax.all_to_all(x, axes, split_axis=0, concat_axis=0, tiled=True)  22.2 us
  transfers between devices with their start and end apart: 1, of which 1 were waited for; matrix products, arithmetic and copies ran while one was open for 0% of the time, Pallas kernels for 0%

profile of v3, /device:TPU:1, one launch (start us, length us, event | category | flops | bytes accessed | tf_op | source)
XLA Modules:
  0.0 341.0 jit_solution(2922064347158851041)
XLA Ops:
  0.6 4.6 %shard_map.77 = bf16[512,3,2,128]{3,2,1,0:T(2,128)(2,1)} custom-call(s32[4]{0:T(128)} %bitcast.6, bf16[1024,512]{1,0:T(8,128)(2,1)} %v_ref.3, bf16[1024,256]{1,0:T(8,128)(2,1)} %start_ref.1), custom_call_target="tpu_custom_call" | custom-call | flops 805306368 | bytes 1048576 | tf_op jit(solution)/shard_map/pallas_call | solution.py:292
  5.3 22.2 %all-to-all-start = ((bf16[512,3,2,128]{3,2,1,0:T(2,128)(2,1)}), bf16[512,3,2,128]{3,2,1,0:T(2,128)(2,1)S(1)}, u32[]{:S(2)}, u32[]{:S(2)}) async-start(bf16[512,3,2,128]{3,2,1,0:T(2,128)(2,1)} %shard_map.77), calls=%async_computation | async-start | bytes 1572864 | tf_op jit(solution)/shard_map/all_to_all | solution.py:273
  27.5 0.8 slice_reduce_fusion.owner_ref.refs_0_
  28.3 26.2 %all-to-all-done.src_ref = bf16[512,3,2,128]{3,2,1,0:T(2,128)(2,1)S(1)} async-done(((bf16[512,3,2,128]{3,2,1,0:T(2,128)(2,1)}), bf16[512,3,2,128]{3,2,1,0:T(2,128)(2,1)S(1)}, u32[]{:S(2)}, u32[]{:S(2)}) %all-to-all-start) | async-done | bytes 786464 | tf_op jit(solution)/shard_map/all_to_all | solution.py:273
  54.4 1.6 shard_map.78
  56.0 37.5 %all_to_all.70.pieces_ref = bf16[512,3,2,128]{3,2,1,0:T(2,128)(2,1)S(1)} all-to-all(bf16[512,3,2,128]{3,2,1,0:T(2,128)(2,1)S(1)} %shard_map.78), channel_id=1, replica_groups=mesh['y'=8,'c'=2,'x'=4,'z'=8] {'y','c','x','z'}, dimensions={0} | all-to-all | bytes 1572864 | tf_op jit(solution)/shard_map/all_to_all | solution.py:273
  93.5 0.9 shard_map.79
  94.4 11.1 %all_to_all.71.got_ref = f32[16,1,128]{2,1,0:T(1,128)S(1)} all-to-all(f32[16,1,128]{2,1,0:T(1,128)S(1)} %get-tuple-element.19), channel_id=1, replica_groups=mesh['y'=8,'c'=2,'x'=4,'z'=8] {'y','c'}, dimensions={0} | all-to-all | bytes 16384 | tf_op jit(solution)/shard_map/all_to_all | solution.py:273
  105.5 12.9 %all_to_all.72.sums_ref.spread_ref = f32[32,1,128]{2,1,0:T(1,128)S(1)} all-to-all(f32[32,1,128]{2,1,0:T(1,128)S(1)} %shard_map.80), channel_id=1, replica_groups=mesh['y'=8,'c'=2,'x'=4,'z'=8] {'x','z'}, dimensions={0} | all-to-all | bytes 32768 | tf_op jit(solution)/shard_map/all_to_all | solution.py:273
  119.0 27.6 %all_to_all.73.refs_2_ = bf16[512,2,128]{2,1,0:T(2,128)(2,1)S(1)} all-to-all(bf16[512,2,128]{2,1,0:T(2,128)(2,1)S(1)} %get-tuple-element.22), channel_id=1, replica_groups=mesh['y'=8,'c'=2,'x'=4,'z'=8] {'y','c','x','z'}, dimensions={0} | all-to-all | bytes 524288 | tf_op jit(solution)/shard_map/all_to_all | solution.py:273
  146.6 1.7 shard_map.82
  148.4 43.0 %all_to_all.74 = bf16[512,8,128]{2,1,0:T(8,128)(2,1)S(1)} all-to-all(bf16[512,8,128]{2,1,0:T(8,128)(2,1)S(1)} %shard_map.82), channel_id=1, replica_groups=mesh['y'=8,'c'=2,'x'=4,'z'=8] {'y','c','x','z'}, dimensions={0} | all-to-all | bytes 2097152 | tf_op jit(solution)/shard_map/all_to_all | solution.py:273
  192.0 2.0 shard_map.83
  194.0 10.7 %all_to_all.75.got_ref = f32[16,1,128]{2,1,0:T(1,128)S(1)} all-to-all(f32[16,1,128]{2,1,0:T(1,128)S(1)} %get-tuple-element.25), channel_id=1, replica_groups=mesh['y'=8,'c'=2,'x'=4,'z'=8] {'y','c'}, dimensions={0} | all-to-all | bytes 16384 | tf_op jit(solution)/shard_map/all_to_all | solution.py:273
  204.7 12.8 %all_to_all.76.sums_ref = f32[32,1,128]{2,1,0:T(1,128)S(1)} all-to-all(f32[32,1,128]{2,1,0:T(1,128)S(1)} %shard_map.84), channel_id=1, replica_groups=mesh['y'=8,'c'=2,'x'=4,'z'=8] {'x','z'}, dimensions={0} | all-to-all | bytes 32768 | tf_op jit(solution)/shard_map/all_to_all | solution.py:273
  218.2 11.6 %all_to_all.77.got_ref = f32[16,1,128]{2,1,0:T(1,128)S(1)} all-to-all(f32[16,1,128]{2,1,0:T(1,128)S(1)} %get-tuple-element.27), channel_id=1, replica_groups=mesh['y'=8,'c'=2,'x'=4,'z'=8] {'y','c'}, dimensions={0} | all-to-all | bytes 16384 | tf_op jit(solution)/shard_map/all_to_all | solution.py:273
  229.8 11.6 %all_to_all.78.sums_ref.spread_ref = f32[32,1,128]{2,1,0:T(1,128)S(1)} all-to-all(f32[32,1,128]{2,1,0:T(1,128)S(1)} %shard_map.86), channel_id=1, replica_groups=mesh['y'=8,'c'=2,'x'=4,'z'=8] {'x','z'}, dimensions={0} | all-to-all | bytes 32768 | tf_op jit(solution)/shard_map/all_to_all | solution.py:273
  242.2 27.3 %all_to_all.79.refs_2_ = bf16[512,2,128]{2,1,0:T(2,128)(2,1)S(1)} all-to-all(bf16[512,2,128]{2,1,0:T(2,128)(2,1)S(1)} %get-tuple-element.29), channel_id=1, replica_groups=mesh['y'=8,'c'=2,'x'=4,'z'=8] {'y','c','x','z'}, dimensions={0} | all-to-all | bytes 524288 | tf_op jit(solution)/shard_map/all_to_all | solution.py:273
  269.5 1.7 shard_map.88
  271.2 42.7 %all_to_all.80 = bf16[512,8,128]{2,1,0:T(8,128)(2,1)S(1)} all-to-all(bf16[512,8,128]{2,1,0:T(8,128)(2,1)S(1)} %shard_map.88), channel_id=1, replica_groups=mesh['y'=8,'c'=2,'x'=4,'z'=8] {'y','c','x','z'}, dimensions={0} | all-to-all | bytes 2097152 | tf_op jit(solution)/shard_map/all_to_all | solution.py:273
  313.9 1.9 shard_map.89
  315.8 10.7 %all_to_all.81.got_ref = f32[16,1,128]{2,1,0:T(1,128)S(1)} all-to-all(f32[16,1,128]{2,1,0:T(1,128)S(1)} %get-tuple-element.31), channel_id=1, replica_groups=mesh['y'=8,'c'=2,'x'=4,'z'=8] {'y','c'}, dimensions={0} | all-to-all | bytes 16384 | tf_op jit(solution)/shard_map/all_to_all | solution.py:273
  326.6 12.8 %all_to_all.82.sums_ref = f32[32,1,128]{2,1,0:T(1,128)S(1)} all-to-all(f32[32,1,128]{2,1,0:T(1,128)S(1)} %shard_map.90), channel_id=1, replica_groups=mesh['y'=8,'c'=2,'x'=4,'z'=8] {'x','z'}, dimensions={0} | all-to-all | bytes 32768 | tf_op jit(solution)/shard_map/all_to_all | solution.py:273
  339.4 1.6 shard_map.91
  (17 shorter events, 2.8 us)
Async XLA Ops:
  5.3 49.2 %all-to-all-start = ((bf16[512,3,2,128]{3,2,1,0:T(2,128)(2,1)}), bf16[512,3,2,128]{3,2,1,0:T(2,128)(2,1)S(1)}, u32[]{:S(2)}, u32[]{:S(2)}) async-start(bf16[512,3,2,128]{3,2,1,0:T(2,128)(2,1)} %shard_map.77), calls=%async_computation | async-start | bytes 1572864 | tf_op jit(solution)/shard_map/all_to_all | solution.py:273
  56.0 37.5 %copy-start = (bf16[1024,512]{1,0:T(8,128)(2,1)S(1)}, bf16[1024,512]{1,0:T(8,128)(2,1)}, u32[]{:S(2)}) copy-start(bf16[1024,512]{1,0:T(8,128)(2,1)} %u_ref.5) | copy-start | bytes 3145732
  56.0 37.5 %copy-start.2 = (bf16[1024,256]{1,0:T(8,128)(2,1)S(1)}, bf16[1024,256]{1,0:T(8,128)(2,1)}, u32[]{:S(2)}) copy-start(bf16[1024,256]{1,0:T(8,128)(2,1)} %observed_ref.1) | copy-start | bytes 1572868
  148.4 43.0 %copy-start.1 = (bf16[1024,512]{1,0:T(8,128)(2,1)S(1)}, bf16[1024,512]{1,0:T(8,128)(2,1)}, u32[]{:S(2)}) copy-start(bf16[1024,512]{1,0:T(8,128)(2,1)} %v_ref.3) | copy-start | bytes 3145732
  191.4 0.7 copy-start.4
  313.9 25.5 %copy-start.3 = (bf16[1024,256]{1,0:T(8,128)(2,1)S(1)}, bf16[1024,256]{1,0:T(8,128)(2,1)}, u32[]{:S(2)}) copy-start(bf16[1024,256]{1,0:T(8,128)(2,1)} %start_ref.1) | copy-start | bytes 1572868

commit v4 on v3

--- a/solution.py
+++ b/solution.py
@@ -65,7 +65,7 @@
     return double_ref[pl.ds(2 * source * inner + ((inner - shift) & (inner - 1)), inner)]
 
 
-def deliver_kernel(outer, inner, owner_ref, here_ref, src_ref, out_ref, double_ref):
+def deliver_kernel(outer, inner, owner_ref, here_ref, src_ref, ranks_ref, out_ref, double_ref):
     owner = owner_ref[here_ref[0]]
     lead, shift = lax.div(owner, inner), lax.rem(owner, inner)
     widen(outer, inner, src_ref, double_ref)
@@ -272,15 +272,15 @@
     def scatter(x, axes):
         return lax.all_to_all(x, axes, split_axis=0, concat_axis=0, tiled=True)
 
-    def route(kernel, pieces, out):
+    def route(kernel, pieces, out, early=()):
         got = scatter(pieces, ALL)
         moved = call(
             functools.partial(kernel, groups, members),
             struct((devices,) + out, BF16),
-            "ssv",
+            "ssv" + "s" * len(early),
             [pltpu.VMEM((2 * devices,) + pieces.shape[1:], BF16)],
             flops=10**8,
-        )(owner, here, got)
+        )(owner, here, got, *early)
         return scatter(moved, ALL)
 
     def total(partial):
@@ -309,7 +309,7 @@
         "vvv",
         [pltpu.VMEM((width, rhs), BF16)],
         flops=flops,
-    )(route(deliver_kernel, pieces, (kinds,) + piece), u_stack, observed)
+    )(route(deliver_kernel, pieces, (kinds,) + piece, (ranks,)), u_stack, observed)
     exchange = lambda outer, inner, *refs: exchange_kernel(outer, inner, slots, *refs)
     earlier = []
     for index in range(ITERS):

time: 342 us -> 341 us (level)
  no operation moved by 1% of the time
where the time goes in v4:
time: 341 us; the launch traced here: 340 us
  blocking collectives  272 us (80%)
  waiting for transfers between devices  26.2 us (8%)
  starting transfers between devices  22.2 us (7%)
  Pallas kernels  18.3 us (5%)
    all_to_all x13, blocking collectives, scatter(): return lax.all_to_all(x, axes, split_axis=0, concat_axis=0, tiled=True)  272 us
    all_to_all x1, waiting for transfers between devices, scatter(): return lax.all_to_all(x, axes, split_axis=0, concat_axis=0, tiled=True)  26.2 us
    all_to_all x1, starting transfers between devices, scatter(): return lax.all_to_all(x, axes, split_axis=0, concat_axis=0, tiled=True)  22.2 us
  transfers between devices with their start and end apart: 1, of which 1 were waited for; matrix products, arithmetic and copies ran while one was open for 0% of the time, Pallas kernels for 0%

profile of v4, /device:TPU:1, one launch (start us, length us, event | category | flops | bytes accessed | tf_op | source)
XLA Modules:
  0.0 340.5 jit_solution(4272620540221158980)
XLA Ops:
  0.6 4.6 %shard_map.77 = bf16[512,3,2,128]{3,2,1,0:T(2,128)(2,1)} custom-call(s32[4]{0:T(128)} %bitcast.6, bf16[1024,512]{1,0:T(8,128)(2,1)} %v_ref.3, bf16[1024,256]{1,0:T(8,128)(2,1)} %start_ref.1), custom_call_target="tpu_custom_call" | custom-call | flops 805306368 | bytes 1048576 | tf_op jit(solution)/shard_map/pallas_call | solution.py:292
  5.3 22.2 %all-to-all-start = ((bf16[512,3,2,128]{3,2,1,0:T(2,128)(2,1)}), bf16[512,3,2,128]{3,2,1,0:T(2,128)(2,1)S(1)}, u32[]{:S(2)}, u32[]{:S(2)}) async-start(bf16[512,3,2,128]{3,2,1,0:T(2,128)(2,1)} %shard_map.77), calls=%async_computation | async-start | bytes 1572864 | tf_op jit(solution)/shard_map/all_to_all | solution.py:273
  27.5 0.8 slice_reduce_fusion.owner_ref.refs_0_
  28.3 26.2 %all-to-all-done.src_ref = bf16[512,3,2,128]{3,2,1,0:T(2,128)(2,1)S(1)} async-done(((bf16[512,3,2,128]{3,2,1,0:T(2,128)(2,1)}), bf16[512,3,2,128]{3,2,1,0:T(2,128)(2,1)S(1)}, u32[]{:S(2)}, u32[]{:S(2)}) %all-to-all-start) | async-done | bytes 786464 | tf_op jit(solution)/shard_map/all_to_all | solution.py:273
  54.4 1.6 shard_map.78
  56.0 37.5 %all_to_all.70.pieces_ref = bf16[512,3,2,128]{3,2,1,0:T(2,128)(2,1)S(1)} all-to-all(bf16[512,3,2,128]{3,2,1,0:T(2,128)(2,1)S(1)} %shard_map.78), channel_id=1, replica_groups=mesh['y'=8,'c'=2,'x'=4,'z'=8] {'y','c','x','z'}, dimensions={0} | all-to-all | bytes 1572864 | tf_op jit(solution)/shard_map/all_to_all | solution.py:273
  93.5 0.9 shard_map.79
  94.4 11.1 %all_to_all.71.got_ref = f32[16,1,128]{2,1,0:T(1,128)S(1)} all-to-all(f32[16,1,128]{2,1,0:T(1,128)S(1)} %get-tuple-element.19), channel_id=1, replica_groups=mesh['y'=8,'c'=2,'x'=4,'z'=8] {'y','c'}, dimensions={0} | all-to-all | bytes 16384 | tf_op jit(solution)/shard_map/all_to_all | solution.py:273
  105.5 12.9 %all_to_all.72.sums_ref.spread_ref = f32[32,1,128]{2,1,0:T(1,128)S(1)} all-to-all(f32[32,1,128]{2,1,0:T(1,128)S(1)} %shard_map.80), channel_id=1, replica_groups=mesh['y'=8,'c'=2,'x'=4,'z'=8] {'x','z'}, dimensions={0} | all-to-all | bytes 32768 | tf_op jit(solution)/shard_map/all_to_all | solution.py:273
  119.0 27.6 %all_to_all.73.refs_2_ = bf16[512,2,128]{2,1,0:T(2,128)(2,1)S(1)} all-to-all(bf16[512,2,128]{2,1,0:T(2,128)(2,1)S(1)} %get-tuple-element.22), channel_id=1, replica_groups=mesh['y'=8,'c'=2,'x'=4,'z'=8] {'y','c','x','z'}, dimensions={0} | all-to-all | bytes 524288 | tf_op jit(solution)/shard_map/all_to_all | solution.py:273
  146.6 1.7 shard_map.82
  148.4 43.0 %all_to_all.74 = bf16[512,8,128]{2,1,0:T(8,128)(2,1)S(1)} all-to-all(bf16[512,8,128]{2,1,0:T(8,128)(2,1)S(1)} %shard_map.82), channel_id=1, replica_groups=mesh['y'=8,'c'=2,'x'=4,'z'=8] {'y','c','x','z'}, dimensions={0} | all-to-all | bytes 2097152 | tf_op jit(solution)/shard_map/all_to_all | solution.py:273
  191.4 2.0 shard_map.83
  193.4 10.7 %all_to_all.75.got_ref = f32[16,1,128]{2,1,0:T(1,128)S(1)} all-to-all(f32[16,1,128]{2,1,0:T(1,128)S(1)} %get-tuple-element.25), channel_id=1, replica_groups=mesh['y'=8,'c'=2,'x'=4,'z'=8] {'y','c'}, dimensions={0} | all-to-all | bytes 16384 | tf_op jit(solution)/shard_map/all_to_all | solution.py:273
  204.2 12.8 %all_to_all.76.sums_ref = f32[32,1,128]{2,1,0:T(1,128)S(1)} all-to-all(f32[32,1,128]{2,1,0:T(1,128)S(1)} %shard_map.84), channel_id=1, replica_groups=mesh['y'=8,'c'=2,'x'=4,'z'=8] {'x','z'}, dimensions={0} | all-to-all | bytes 32768 | tf_op jit(solution)/shard_map/all_to_all | solution.py:273
  217.7 11.6 %all_to_all.77.got_ref = f32[16,1,128]{2,1,0:T(1,128)S(1)} all-to-all(f32[16,1,128]{2,1,0:T(1,128)S(1)} %get-tuple-element.27), channel_id=1, replica_groups=mesh['y'=8,'c'=2,'x'=4,'z'=8] {'y','c'}, dimensions={0} | all-to-all | bytes 16384 | tf_op jit(solution)/shard_map/all_to_all | solution.py:273
  229.3 11.6 %all_to_all.78.sums_ref.spread_ref = f32[32,1,128]{2,1,0:T(1,128)S(1)} all-to-all(f32[32,1,128]{2,1,0:T(1,128)S(1)} %shard_map.86), channel_id=1, replica_groups=mesh['y'=8,'c'=2,'x'=4,'z'=8] {'x','z'}, dimensions={0} | all-to-all | bytes 32768 | tf_op jit(solution)/shard_map/all_to_all | solution.py:273
  241.6 27.3 %all_to_all.79.refs_2_ = bf16[512,2,128]{2,1,0:T(2,128)(2,1)S(1)} all-to-all(bf16[512,2,128]{2,1,0:T(2,128)(2,1)S(1)} %get-tuple-element.29), channel_id=1, replica_groups=mesh['y'=8,'c'=2,'x'=4,'z'=8] {'y','c','x','z'}, dimensions={0} | all-to-all | bytes 524288 | tf_op jit(solution)/shard_map/all_to_all | solution.py:273
  268.9 1.7 shard_map.88
  270.6 42.7 %all_to_all.80 = bf16[512,8,128]{2,1,0:T(8,128)(2,1)S(1)} all-to-all(bf16[512,8,128]{2,1,0:T(8,128)(2,1)S(1)} %shard_map.88), channel_id=1, replica_groups=mesh['y'=8,'c'=2,'x'=4,'z'=8] {'y','c','x','z'}, dimensions={0} | all-to-all | bytes 2097152 | tf_op jit(solution)/shard_map/all_to_all | solution.py:273
  313.3 2.0 shard_map.89
  315.3 10.7 %all_to_all.81.got_ref = f32[16,1,128]{2,1,0:T(1,128)S(1)} all-to-all(f32[16,1,128]{2,1,0:T(1,128)S(1)} %get-tuple-element.31), channel_id=1, replica_groups=mesh['y'=8,'c'=2,'x'=4,'z'=8] {'y','c'}, dimensions={0} | all-to-all | bytes 16384 | tf_op jit(solution)/shard_map/all_to_all | solution.py:273
  326.1 12.8 %all_to_all.82.sums_ref = f32[32,1,128]{2,1,0:T(1,128)S(1)} all-to-all(f32[32,1,128]{2,1,0:T(1,128)S(1)} %shard_map.90), channel_id=1, replica_groups=mesh['y'=8,'c'=2,'x'=4,'z'=8] {'x','z'}, dimensions={0} | all-to-all | bytes 32768 | tf_op jit(solution)/shard_map/all_to_all | solution.py:273
  338.9 1.6 shard_map.91
  (17 shorter events, 2.2 us)
Async XLA Ops:
  5.3 49.2 %all-to-all-start = ((bf16[512,3,2,128]{3,2,1,0:T(2,128)(2,1)}), bf16[512,3,2,128]{3,2,1,0:T(2,128)(2,1)S(1)}, u32[]{:S(2)}, u32[]{:S(2)}) async-start(bf16[512,3,2,128]{3,2,1,0:T(2,128)(2,1)} %shard_map.77), calls=%async_computation | async-start | bytes 1572864 | tf_op jit(solution)/shard_map/all_to_all | solution.py:273
  28.3 26.2 %copy-start.4 = (s32[1,4]{1,0:T(1,128)S(1)}, s32[1,4]{1,0:T(1,128)}, u32[]{:S(2)}) copy-start(s32[1,4]{1,0:T(1,128)} %param.11) | copy-start | bytes 52
  56.0 37.5 %copy-start = (bf16[1024,512]{1,0:T(8,128)(2,1)S(1)}, bf16[1024,512]{1,0:T(8,128)(2,1)}, u32[]{:S(2)}) copy-start(bf16[1024,512]{1,0:T(8,128)(2,1)} %u_ref.5) | copy-start | bytes 3145732
  56.0 37.5 %copy-start.2 = (bf16[1024,256]{1,0:T(8,128)(2,1)S(1)}, bf16[1024,256]{1,0:T(8,128)(2,1)}, u32[]{:S(2)}) copy-start(bf16[1024,256]{1,0:T(8,128)(2,1)} %observed_ref.1) | copy-start | bytes 1572868
  148.4 43.0 %copy-start.1 = (bf16[1024,512]{1,0:T(8,128)(2,1)S(1)}, bf16[1024,512]{1,0:T(8,128)(2,1)}, u32[]{:S(2)}) copy-start(bf16[1024,512]{1,0:T(8,128)(2,1)} %v_ref.3) | copy-start | bytes 3145732
  313.3 25.6 %copy-start.3 = (bf16[1024,256]{1,0:T(8,128)(2,1)S(1)}, bf16[1024,256]{1,0:T(8,128)(2,1)}, u32[]{:S(2)}) copy-start(bf16[1024,256]{1,0:T(8,128)(2,1)} %start_ref.1) | copy-start | bytes 1572868
